TPU v7x, 32 devices: a whole 2x2x4 slice. The times are simulated.
32 devices in a mesh: batch: 8 (over z, y), ctx: 4 (over x, core).
Axes of the slice: x: 2, y: 2, z: 4, core: 2. Of those that a mesh axis runs over, the one named last changes fastest.
Arguments:
- asked_for: bfloat16 [16, 1024, 16, 128], P('batch', 'ctx'), may hold values from -6 to 6
- offered: bfloat16 [16, 1024, 16, 128], P('batch', 'ctx'), may hold values from -6 to 6
- contents: bfloat16 [16, 1024, 16, 128], P('batch', 'ctx'), may hold values from -6 to 6
- gate_rows: bfloat16 [16, 1024, 16, 128], P('batch', 'ctx'), may hold values from -6 to 6
- out_weight: bfloat16 [2048, 2048], P('batch'), may hold values from -0.125 to 0.125
Outputs:
- block_out: bfloat16 [16, 1024, 2048], P('batch', 'ctx')
All inputs are finite; a program needn't handle non-finite values.
Results may differ from a plain program's by a relative error of at most 0.006.
Values may be sent and summed in bfloat16 or wider, within the bound.
A program may use at most 128 MiB of HBM per device.

v0:
```python
import jax
import jax.numpy as jnp
from jax import lax
from jax.sharding import PartitionSpec as P


def to_features(values):
    wide = values.astype(jnp.float32)
    return jnp.where(wide > 0.0, wide + 1.0, jnp.exp(jnp.minimum(wide, 0.0))).astype(jnp.bfloat16)


def close_heads(read, gate_rows, count):
    result = read * count**0.5
    result = result * jax.nn.sigmoid(gate_rows.astype(jnp.float32))
    return result.astype(jnp.bfloat16)


def ask_state(features, state, mass):
    top = jnp.einsum(
        "bthd,bhde->bthe", features, state.astype(jnp.bfloat16), preferred_element_type=jnp.float32
    )
    bottom = jnp.einsum(
        "bthd,bhd->bth", features.astype(jnp.float32), mass, precision=lax.Precision.HIGHEST
    )
    return top / (bottom + 0.001)[..., None]


def local(asked_for, offered, contents, gate_rows, out_weight):
    query_feature, key_feature = (to_features(asked_for), to_features(offered))
    count = asked_for.shape[1] * lax.axis_size("ctx")
    part_state = jnp.einsum(
        "bthd,bthe->bhde", key_feature, contents, preferred_element_type=jnp.float32
    )
    part_mass = jnp.sum(key_feature.astype(jnp.float32), axis=1)
    state, mass = lax.psum((part_state, part_mass), "ctx")
    read = ask_state(query_feature, state / count, mass / count)
    mixed = close_heads(read, gate_rows, count)
    mixed = mixed.reshape(mixed.shape[0], mixed.shape[1], -1)
    return jnp.einsum(
        "btw,wv->btv",
        mixed,
        lax.all_gather(out_weight, "batch", axis=0, tiled=True),
        preferred_element_type=jnp.float32,
    ).astype(jnp.bfloat16)


def solution(mesh):
    return jax.shard_map(
        local,
        mesh=mesh,
        in_specs=(
            P("batch", "ctx", None, None),
            P("batch", "ctx", None, None),
            P("batch", "ctx", None, None),
            P("batch", "ctx", None, None),
            P("batch", None),
        ),
        out_specs=P("batch", "ctx", None),
        check_vma=False,
    )
```

profile of v0, /device:TPU:0, one launch (start us, length us, event | category | flops | bytes accessed | tf_op | source)
XLA Modules:
  0.0 163.2 jit_solution(13875019643667994663)
XLA Ops:
  7.4 0.0 copy-start
  7.4 0.0 all-reduce.2.cloned.1.call-start
  7.4 4.5 %copy.6 = bf16[2,256,16,128]{1,3,2,0:T(8,128)(2,1)} copy(bf16[2,256,16,128]{3,2,1,0:T(8,128)(2,1)} %param.6) | data formatting | bytes 4194304 | tf_op args[1]
  11.8 0.0 copy-done
  11.8 4.5 %fusion.14 = f32[2,16,128,128]{2,3,1,0:T(8,128)} fusion(bf16[2,256,16,128]{3,2,1,0:T(8,128)(2,1)S(1)} %copy-done, bf16[2,256,16,128]{1,3,2,0:T(8,128)(2,1)} %copy.6), kind=kOutput, calls=%fused_computation.20 | convolution fusion | flops 274726912 | bytes 6291456 | tf_op jit(solution)/shard_map/bthd,bthe->bhde/dot_general | solution.py:31
  16.3 0.0 all-reduce.2.cloned.1.call-update
  16.3 0.0 all-gather.2.cloned.1.call-start
  16.4 0.5 all-gather.2.cloned.1.call-update
  16.9 4.3 %copy.7 = bf16[2,256,16,128]{1,3,2,0:T(8,128)(2,1)} copy(bf16[2,256,16,128]{3,2,1,0:T(8,128)(2,1)} %param.5) | data formatting | bytes 4194304 | tf_op args[0]
  21.2 4.3 %copy.9 = bf16[2,256,16,128]{1,3,2,0:T(8,128)(2,1)} copy(bf16[2,256,16,128]{3,2,1,0:T(8,128)(2,1)} %param.8) | data formatting | bytes 4194304 | tf_op args[3]
  25.5 2.8 %convert_reduce_fusion = f32[2,16,128]{2,1,0:T(8,128)S(1)} fusion(bf16[2,256,16,128]{1,3,2,0:T(8,128)(2,1)} %copy.6), kind=kLoop, calls=%fused_computation.18 | loop fusion | flops 8384512 | bytes 2113536 | tf_op jit(solution)/shard_map/reduce_sum | solution.py:34
  28.3 14.1 %psum.15 = f32[2,16,128]{2,1,0:T(8,128)S(1)} all-reduce(f32[2,16,128]{2,1,0:T(8,128)S(1)} %convert_reduce_fusion), channel_id=1, replica_groups=mesh['batch'=8,'ctx'=4] {'ctx'}, use_global_device_ids=true, to_apply=%region_2.3 | all-reduce | flops 4096 | bytes 32768 | tf_op jit(solution)/shard_map/psum | solution.py:35
  42.4 3.3 %fusion.18 = f32[2,16,1,256]{3,2,1,0:T(1,128)S(1)} fusion(f32[2,16,128,1]{2,3,1,0:T(1,128)S(1)} %bitcast.25, bf16[2,256,16,128]{1,3,2,0:T(8,128)(2,1)} %copy.7), kind=kOutput, calls=%fused_computation.24 | convolution fusion | flops 18874368 | bytes 2146304 | tf_op jit(solution)/shard_map/bthd,bhd->bth/dot_general | solution.py:22
  45.7 25.2 %all-reduce.2.cloned.1.call-done = f32[2,16,128,128]{2,3,1,0:T(8,128)} async-done(((f32[2,16,128,128]{2,3,1,0:T(8,128)}), f32[2,16,128,128]{2,3,1,0:T(8,128)}) %all-reduce.2.cloned.1.call-update) | async-done | bytes 2097168 | tf_op jit(solution)/shard_map/psum | solution.py:35
  70.9 7.2 %fusion.10 = bf16[2,256,16,128]{1,3,2,0:T(8,128)(2,1)} fusion(bf16[2,256,16,128]{1,3,2,0:T(8,128)(2,1)} %copy.9, f32[2,256,16]{1,2,0:T(8,128)S(1)} %fusion.21, f32[2,16,128,128]{2,3,1,0:T(8,128)} %all-reduce.2.cloned.1.call-done, bf16[2,256,16,128]{1,3,2,0:T(8,128)(2,1)} %copy.7), kind=kOutput, calls=%fused_computation.17 | convolution fusion | flops 284164096 | bytes 8421376 | tf_op jit(solution)/shard_map/bthd,bhde->bthe/dot_general | solution.py:19
  78.1 67.8 %all-gather.2.cloned.1.call-done = bf16[2048,2048]{1,0:T(8,128)(2,1)} async-done(((bf16[256,2048]{1,0:T(8,128)(2,1)}), bf16[2048,2048]{1,0:T(8,128)(2,1)}) %all-gather.2.cloned.1.call-update) | async-done | bytes 8388624 | tf_op jit(solution)/shard_map/all_gather | solution.py:42
  145.9 9.9 %fusion.11 = bf16[2,256,2048]{2,1,0:T(8,128)(2,1)} fusion(bf16[2,256,2048]{1,2,0:T(8,128)(2,1)} %bitcast.26, bf16[2048,2048]{1,0:T(8,128)(2,1)} %all-gather.2.cloned.1.call-done), kind=kOutput, calls=%fused_computation.19 | convolution fusion | flops 4296015872 | bytes 12582912 | tf_op jit(solution)/shard_map/btw,wv->btv/dot_general | solution.py:39
  (2 shorter events, 0.0 us)
Async XLA Ops:
  7.4 4.5 %copy-start = (bf16[2,256,16,128]{3,2,1,0:T(8,128)(2,1)S(1)}, bf16[2,256,16,128]{3,2,1,0:T(8,128)(2,1)}, u32[]{:S(2)}) copy-start(bf16[2,256,16,128]{3,2,1,0:T(8,128)(2,1)} %param.7) | copy-start | bytes 6291460
  7.4 63.5 %all-reduce.2.cloned.1.call-start = ((), (), s32[]{:S(2)}) async-start(), calls=%async_computation | async-start | bytes 4194304 | tf_op jit(solution)/shard_map/psum | solution.py:35
  16.3 129.5 %all-gather.2.cloned.1.call-start = ((), (), s32[]{:S(2)}) async-start(), calls=%async_computation.1 | async-start | bytes 9437184 | tf_op jit(solution)/shard_map/all_gather | solution.py:42
Sparse Core Ops, SparseCore 0:
  16.5 54.3 all-reduce.1
Sparse Core Ops, SparseCore 1:
  19.0 126.9 all-gather.1
where the time goes:
time: 164 us; the launch traced here: 163 us
  waiting for transfers between devices  93.5 us (57%)
  matrix products  24.9 us (15%)
  between operations  14.9 us (9%)
  blocking collectives  14.1 us (9%)
  local copies, waits for them, and re-layouts  13 us (8%)
  other arithmetic  2.77 us (2%)
    all_gather x1, waiting for transfers between devices, local(): lax.all_gather(out_weight, 'batch', axis=0, tiled=True)  67.8 us
    psum x1, waiting for transfers between devices, local(): state, mass = lax.psum((part_state, part_mass), 'ctx')  25.2 us
    psum x1, blocking collectives, local(): state, mass = lax.psum((part_state, part_mass), 'ctx')  14.1 us
    unnamed x5, local copies, waits for them, and re-layouts  13 us
    dot_general x1, matrix products, local(): jnp.einsum('btw,wv->btv', mixed, lax.all_gather(out_weight, 'batch', axis...  9.9 us
    dot_general x1, matrix products, ask_state(): jnp.einsum('bthd,bhde->bthe', features, state.astype(jnp.bfloat16), prefe...  7.2 us
    dot_general x1, matrix products, local(): jnp.einsum('bthd,bthe->bhde', key_feature, contents, preferred_element_ty...  4.48 us
    dot_general x1, matrix products, ask_state(): jnp.einsum('bthd,bhd->bth', features.astype(jnp.float32), mass, precision...  3.29 us
  transfers between devices with their start and end apart: 2, of which 2 were waited for; matrix products, arithmetic and copies ran while one was open for 13% of the time, Pallas kernels for 0%

commit v1 on v0

v1 whole, which is shorter than its diff:
```python
import functools

import jax
import jax.numpy as jnp
from jax import lax
from jax.experimental import pallas as pl
from jax.experimental.pallas import tpu as pltpu
from jax.sharding import PartitionSpec as P

MESH = pl.DeviceIdType.MESH
CORES = 2
BF16, F32 = jnp.bfloat16, jnp.float32


def ring_place(block, n):
    odd = lax.rem(block, 2)
    half = block // 2
    return (1 - odd) * half + odd * (n - 1 - half)


def ring_block(place, n):
    late = place // ((n + 1) // 2)
    return (1 - late) * (2 * place) + late * (2 * (n - 1 - place) + 1)


def features(wide):
    return jnp.where(wide > 0.0, wide + 1.0, jnp.exp(jnp.minimum(wide, 0.0))).astype(BF16).astype(F32)


def kernel(
    n, members, shared,
    q_hbm, k_hbm, v_hbm, g_hbm, w_hbm, out_hbm,
    q_in, k_in, v_in, g_in, kn, vn, qn, gn,
    part_send, part_own, part_recv, mass_send, mass_own, mass_recv,
    far_send, far_recv, mass_far_send, mass_far_recv, state, mass, state_in, mass_in,
    weight, mixed, acc, out_vm,
    in_sem, out_sem, ring_send, ring_recv, mate_send, mate_recv, far_w_send, far_w_recv,
    part_ss, part_rs, far_ss, far_rs, fin_ss, fin_rs,
):
    batch, tokens, heads, size = q_in.shape
    rows, width = weight.shape[1:]
    planes = members // CORES
    count = tokens * members
    halves = batch // CORES
    b, c = lax.axis_index("batch"), lax.axis_index("ctx")
    core, plane = lax.rem(c, CORES), c // CORES
    mate = plane * CORES + (1 - core)
    p = ring_place(b, n)
    turn = 1 - 2 * core
    nxt = ring_block(lax.rem(p + turn + n, n), n)
    prv = ring_block(lax.rem(p - turn + n, n), n)

    def far(d):
        return lax.rem(plane + d, planes) * CORES + core

    loads = [
        pltpu.make_async_copy(src, dst, in_sem.at[i])
        for i, (src, dst) in enumerate(
            [(w_hbm, weight.at[b]), (k_hbm, k_in), (v_hbm, v_in), (q_hbm, q_in), (g_hbm, g_in)]
        )
    ]
    for load in loads:
        load.start()

    barrier = pltpu.get_barrier_semaphore()
    peers = [{"batch": nxt, "ctx": c}, {"batch": prv, "ctx": c}, {"batch": b, "ctx": mate}]
    peers += [{"batch": b, "ctx": far(d)} for d in range(1, planes)]
    for peer in peers:
        pl.semaphore_signal(barrier, inc=1, device_id=peer, device_id_type=MESH)
    pl.semaphore_wait(barrier, len(peers))

    rest = (rows - planes * CORES * shared) // CORES
    base = planes * CORES * shared + core * rest
    sizes = ([shared] if shared else []) + [rest // 2, rest // 2]
    offsets = ([(plane * CORES + core) * shared] if shared else []) + [base, base + rest // 2]
    pieces = len(sizes)

    def piece(block, j):
        align = 16
        return weight.at[block, pl.ds(pl.multiple_of(offsets[j], align), sizes[j])]

    def copy(ref, send, recv, peer, dst=None):
        return pltpu.make_async_remote_copy(
            src_ref=ref, dst_ref=ref if dst is None else dst, send_sem=send, recv_sem=recv,
            device_id=peer, device_id_type=MESH,
        )

    def held(s):
        return ring_block(lax.rem(p - turn * (s + 1) + n, n), n)

    to_next, to_mate = {"batch": nxt, "ctx": c}, {"batch": b, "ctx": mate}
    sent = []

    def send(*args, **kw):
        one = copy(*args, **kw)
        one.start()
        sent.append(one)

    loads[0].wait()
    for j in range(pieces):
        send(piece(b, j), ring_send.at[0, j], ring_recv.at[0, j], to_next)

    steps = n - 1
    order = [(s, j) for s in range(steps) for j in range(pieces)]
    done = [0]
    crossed = [0]

    def ring_event(s, j):
        part = piece(held(s), j)
        copy(part, ring_send.at[s, j], ring_recv.at[s, j], to_next).wait_recv()
        if s + 1 < steps:
            send(part, ring_send.at[s + 1, j], ring_recv.at[s + 1, j], to_next)
        if shared and j == 0:
            for d in range(1, planes):
                send(part, far_w_send.at[s, d - 1], far_w_recv.at[s, d - 1], {"batch": b, "ctx": far(d)})
        send(part, mate_send.at[s, j], mate_recv.at[s, j], to_mate)

    def pump(k):
        for s, j in order[done[0] : done[0] + k]:
            ring_event(s, j)
        done[0] += k

    def pump_to(s, j):
        target = s * pieces + j + 1
        if target > done[0]:
            pump(min(target, len(order)) - done[0])

    def cross_to(s):
        while shared and crossed[0] <= min(s, steps - 1):
            s_now = crossed[0]
            for d in range(1, planes):
                other = lax.rem(plane - d + planes, planes)
                at = pl.multiple_of((other * CORES + core) * shared, 16)
                ref = weight.at[held(s_now), pl.ds(at, shared)]
                copy(ref, far_w_send.at[s_now, d - 1], far_w_recv.at[s_now, d - 1], {"batch": b, "ctx": far(d)}).wait_recv()
                slot = pieces + d - 1
                send(ref, mate_send.at[s_now, slot], mate_recv.at[s_now, slot], to_mate)
            crossed[0] += 1

    waited = [0]

    def mate_to(s):
        while waited[0] <= s:
            s_now = waited[0]
            for j in range(pieces):
                ref = weight.at[0, pl.ds(0, sizes[j])]
                copy(ref, mate_send.at[s_now, j], mate_recv.at[s_now, j], to_mate).wait_recv()
            if shared:
                for d in range(1, planes):
                    ref = weight.at[0, pl.ds(0, shared)]
                    slot = pieces + d - 1
                    copy(ref, mate_send.at[s_now, slot], mate_recv.at[s_now, slot], to_mate).wait_recv()
            waited[0] += 1

    chunk = 16

    def spread(src, seq, dst, at, fn):
        def one(i, _):
            t = pl.multiple_of(i * chunk, chunk)
            wide = fn(src[seq, pl.ds(t, chunk)].astype(F32))
            where = pl.multiple_of(at + t * heads, chunk * heads)
            dst[pl.ds(where, chunk * heads), :] = wide.reshape(chunk * heads, size)
            return 0

        lax.fori_loop(0, tokens // chunk, one, 0)

    group = 8
    per_seq = heads // group
    groups = halves * per_seq

    def one_group(part, masses, g):
        h0 = (g % per_seq) * group
        for i in range(group):
            k = kn[pl.ds(h0 + i, tokens, stride=heads), :]
            v = vn[pl.ds(h0 + i, tokens, stride=heads), :]
            part[g * group + i] = lax.dot_general(
                k.astype(BF16), v.astype(BF16), (((0,), (0,)), ((), ())), preferred_element_type=F32
            )
            masses[g, i : i + 1, :] = jnp.sum(k, axis=0, keepdims=True)

    loads[1].wait()
    loads[2].wait()
    for g in range(groups):
        if g % per_seq == 0:
            seq = (1 - core) * halves + g // per_seq
            spread(k_in, seq, kn, 0, features)
            spread(v_in, seq, vn, 0, lambda x: x)
        one_group(part_send, mass_send, g)
        span = pl.ds(g * group, group)
        send(part_send.at[span], part_ss.at[g, 0], part_rs.at[g, 0], to_mate, dst=part_recv.at[span])
        send(mass_send.at[g], part_ss.at[g, 1], part_rs.at[g, 1], to_mate, dst=mass_recv.at[g])
    for g in range(groups):
        if g % per_seq == 0:
            seq = core * halves + g // per_seq
            spread(k_in, seq, kn, 0, features)
            spread(v_in, seq, vn, 0, lambda x: x)
        one_group(part_own, mass_own, g)
        span = pl.ds(g * group, group)
        copy(part_send.at[span], part_ss.at[g, 0], part_rs.at[g, 0], to_mate, dst=part_recv.at[span]).wait_recv()
        copy(mass_send.at[g], part_ss.at[g, 1], part_rs.at[g, 1], to_mate, dst=mass_recv.at[g]).wait_recv()
        for i in range(g * group, (g + 1) * group):
            total = part_own[i] + part_recv[i]
            part_own[i] = total
            far_send[i] = total.astype(BF16)
        total = mass_own[g] + mass_recv[g]
        mass_own[g] = total
        mass_far_send[g] = total
        for d in range(1, planes):
            peer = {"batch": b, "ctx": far(d)}
            send(far_send.at[span], far_ss.at[g, d - 1, 0], far_rs.at[g, d - 1, 0], peer, dst=far_recv.at[d - 1, span])
            send(mass_far_send.at[g], far_ss.at[g, d - 1, 1], far_rs.at[g, d - 1, 1], peer, dst=mass_far_recv.at[d - 1, g])
        pump(1)

    loads[3].wait()
    for seq in range(batch):
        spread(q_in, seq, qn, seq * tokens * heads, features)
        pump(1)
    loads[4].wait()
    for seq in range(batch):
        spread(g_in, seq, gn, seq * tokens * heads, lambda x: 1.0 + jnp.exp(-x))
        pump(1)
    pump_to((n - 1) // 2, 0)

    scale = 1.0 / count
    for g in range(groups):
        span = pl.ds(g * group, group)
        for d in range(1, planes):
            peer = {"batch": b, "ctx": far(d)}
            copy(far_send.at[span], far_ss.at[g, d - 1, 0], far_rs.at[g, d - 1, 0], peer, dst=far_recv.at[d - 1, span]).wait_recv()
            copy(mass_far_send.at[g], far_ss.at[g, d - 1, 1], far_rs.at[g, d - 1, 1], peer, dst=mass_far_recv.at[d - 1, g]).wait_recv()
        for i in range(g * group, (g + 1) * group):
            total = part_own[i]
            for d in range(1, planes):
                total = total + far_recv[d - 1, i].astype(F32)
            state[i] = (total * scale).astype(BF16)
        total = mass_own[g]
        for d in range(1, planes):
            total = total + mass_far_recv[d - 1, g]
        mass[g] = total * scale
        send(state.at[span], fin_ss.at[g, 0], fin_rs.at[g, 0], to_mate, dst=state_in.at[span])
        send(mass.at[g], fin_ss.at[g, 1], fin_rs.at[g, 1], to_mate, dst=mass_in.at[g])

    per_block = rows // size

    def answer(state_ref, mass_ref, g, owner):
        seq = owner * halves + g // per_seq
        h0 = (g % per_seq) * group
        for i in range(group):
            h = h0 + i
            at = seq * (tokens * heads) + h
            ask = qn[pl.ds(at, tokens, stride=heads), :].astype(BF16)
            close = gn[pl.ds(at, tokens, stride=heads), :]
            top = jnp.dot(ask, state_ref[g * group + i], preferred_element_type=F32)
            row = mass_ref[g, i : i + 1, :]
            high = row.astype(BF16).astype(F32)
            both = jnp.concatenate([high, row - high], axis=1)
            both = jnp.broadcast_to(both, (size, 2 * size)).astype(BF16)
            bottom = lax.dot_general(
                jnp.concatenate([ask, ask], axis=1), both, (((1,), (1,)), ((), ())), preferred_element_type=F32
            )
            value = (top * count**0.5) / ((bottom + 1e-3) * close)
            lane = (h % per_block) * size
            where = pl.ds(pl.multiple_of(seq * tokens, tokens), tokens)
            mixed[h // per_block, where, lane : lane + size] = value.astype(BF16)

    for g in range(groups):
        answer(state, mass, g, core)
        pump(1)
    for g in range(groups):
        span = pl.ds(g * group, group)
        copy(state.at[span], fin_ss.at[g, 0], fin_rs.at[g, 0], to_mate, dst=state_in.at[span]).wait_recv()
        copy(mass.at[g], fin_ss.at[g, 1], fin_rs.at[g, 1], to_mate, dst=mass_in.at[g]).wait_recv()
        answer(state_in, mass_in, g, 1 - core)
        pump(1)

    if n % 2 == 0:
        sets = [(0, n // 2)] + [(n // 2 - i, n // 2 + i) for i in range(1, n // 2)]
    else:
        sets = [(0,)] + [(n // 2 + 1 - i, n // 2 + i) for i in range(1, n // 2 + 1)]
    tile = min(512, width)
    tiles = width // tile

    outs = []
    for which, offs in enumerate(sets):
        s = max(max(k, n - k) for k in offs if k) - 1 if any(offs) else -1
        pump_to(s + 1, 0)
        cross_to(s)
        pump_to(s + 1, 1)
        mate_to(s)
        blocks = [ring_block(lax.rem(p - turn * k + n, n), n) for k in offs]
        last = which == len(sets) - 1

        def column(at):
            cols = pl.ds(at, tile)
            left = jnp.concatenate([mixed[i] for i in blocks], axis=1)
            right = jnp.concatenate([weight[i, :, cols] for i in blocks], axis=0)
            made = jnp.dot(left, right, preferred_element_type=F32)
            if which:
                made = made + acc[:, cols]
            if last:
                out_vm[:, cols] = made.astype(BF16)
            else:
                acc[:, cols] = made

        if last:
            for t in range(tiles):
                column(t * tile)
                for seq in range(batch):
                    one = pltpu.make_async_copy(
                        out_vm.at[pl.ds(seq * tokens, tokens), pl.ds(t * tile, tile)],
                        out_hbm.at[seq, :, pl.ds(t * tile, tile)],
                        out_sem.at[t, seq],
                    )
                    one.start()
                    outs.append(one)
        else:
            lax.fori_loop(0, tiles, lambda t, _: (column(pl.multiple_of(t * tile, tile)), 0)[1], 0)
    for one in sent:
        one.wait_send()
    for one in outs:
        one.wait()


def solution(mesh):
    n, members = mesh.shape["batch"], mesh.shape["ctx"]
    planes = members // CORES

    def local(asked_for, offered, contents, gate_rows, out_weight):
        batch, tokens, heads, size = asked_for.shape
        rows, width = out_weight.shape
        shared = rows // 8 if planes == 2 else 0
        pieces = 3 if shared else 2
        half = batch * heads // CORES
        groups = half // 8
        slots = pieces + (planes - 1 if shared else 0)
        vm, dma = pltpu.VMEM, pltpu.SemaphoreType.DMA
        far = max(planes - 1, 1)
        whole = (batch, tokens, heads, size)
        flat = batch * tokens
        tiles = width // min(512, width)
        return pl.pallas_call(
            functools.partial(kernel, n, members, shared),
            out_shape=jax.ShapeDtypeStruct((batch, tokens, width), BF16),
            in_specs=[pl.BlockSpec(memory_space=pl.ANY)] * 5,
            out_specs=pl.BlockSpec(memory_space=pl.ANY),
            scratch_shapes=[
                vm(whole, BF16), vm(whole, BF16), vm(whole, BF16), vm(whole, BF16),
                vm((tokens * heads, size), F32), vm((tokens * heads, size), F32),
                vm((flat * heads, size), F32), vm((flat * heads, size), F32),
                vm((half, size, size), F32), vm((half, size, size), F32), vm((half, size, size), F32),
                vm((groups, 8, size), F32), vm((groups, 8, size), F32), vm((groups, 8, size), F32),
                vm((half, size, size), BF16), vm((far, half, size, size), BF16),
                vm((groups, 8, size), F32), vm((far, groups, 8, size), F32),
                vm((half, size, size), BF16), vm((groups, 8, size), F32),
                vm((half, size, size), BF16), vm((groups, 8, size), F32),
                vm((n, rows, width), BF16),
                vm((n, flat, rows), BF16),
                vm((flat, width), F32),
                vm((flat, width), BF16),
                dma((5,)), dma((tiles, batch)),
                dma((n - 1, pieces)), dma((n - 1, pieces)),
                dma((n - 1, slots)), dma((n - 1, slots)),
                dma((n - 1, far)), dma((n - 1, far)),
                dma((groups, 2)), dma((groups, 2)),
                dma((groups, far, 2)), dma((groups, far, 2)),
                dma((groups, 2)), dma((groups, 2)),
            ],
            compiler_params=pltpu.CompilerParams(
                collective_id=0, has_side_effects=True, vmem_limit_bytes=60 * 1024 * 1024
            ),
        )(asked_for, offered, contents, gate_rows, out_weight)

    return jax.shard_map(
        local,
        mesh=mesh,
        in_specs=(
            P("batch", "ctx", None, None),
            P("batch", "ctx", None, None),
            P("batch", "ctx", None, None),
            P("batch", "ctx", None, None),
            P("batch", None),
        ),
        out_specs=P("batch", "ctx", None),
        check_vma=False,
    )
```

time: 164 us -> 54.2 us (0.33)
  waiting for transfers between devices: 93.5 us -> 0 us
  Pallas kernels: 0 us -> 50.9 us
  matrix products: 24.9 us -> 0 us
  between operations: 14.9 us -> 0.01 us
  blocking collectives: 14.1 us -> 0 us
  local copies, waits for them, and re-layouts: 13 us -> 3.16 us
  other arithmetic: 2.77 us -> 0 us
    all_gather x1 -> x0, waiting for transfers between devices: 67.8 us -> none  [local(): lax.all_gather(out_weight, 'batch', axis=0, tiled=True)]
    pallas_call x0 -> x1, Pallas kernels: none -> 50.9 us  [local(): pl.pallas_call(functools.partial(kernel, n, members, shared), out_shape=j...]
    psum x1 -> x0, waiting for transfers between devices: 25.2 us -> none  [local(): state, mass = lax.psum((part_state, part_mass), 'ctx')]
    dot_general x4 -> x0, matrix products: 24.9 us -> none  [the longest x1 9.9 us: local(): jnp.einsum('btw,wv->btv', mixed, lax.all_gather(out_weight, 'batch', axis...]
    psum x1 -> x0, blocking collectives: 14.1 us -> none  [local(): state, mass = lax.psum((part_state, part_mass), 'ctx')]
    unnamed x5 -> x1, local copies, waits for them, and re-layouts: 13 us -> 3.16 us
    reduce_sum x1 -> x0, other arithmetic: 2.76 us -> none  [local(): part_mass = jnp.sum(key_feature.astype(jnp.float32), axis=1)]
  transfers between devices with their start and end apart: 2 -> 0, of which waited for: 2 -> 0; matrix products, arithmetic and copies ran while one was open for 13% -> 0% of each run, Pallas kernels for 0% -> 0%
where the time goes in v1:
time: 54.2 us; the launch traced here: 54.1 us
  Pallas kernels  50.9 us (94%)
  local copies, waits for them, and re-layouts  3.16 us (6%)
    pallas_call x1, Pallas kernels, local(): pl.pallas_call(functools.partial(kernel, n, members, shared), out_shape=j...  50.9 us
    unnamed x1, local copies, waits for them, and re-layouts  3.16 us

profile of v1, /device:TPU:0, one launch (start us, length us, event | category | flops | bytes accessed | tf_op | source)
XLA Modules:
  0.0 54.1 jit_solution(11953288653409934254)
XLA Ops:
  0.0 50.9 %shard_map.55 = bf16[2,256,2048]{2,1,0:T(8,128)(2,1)} custom-call(bf16[2,256,16,128]{3,2,1,0:T(8,128)(2,1)} %q_hbm.1, bf16[2,256,16,128]{3,2,1,0:T(8,128)(2,1)} %k_hbm.1, bf16[2,256,16,128]{3,2,1,0:T(8,128)(2,1)} %v_hbm.1, bf16[2,256,16,128]{3,2,1,0:T(8,128)(2,1)} %g_hbm.1, bf16[256,2048]{1,0:T(8,128)(2,1)} %w_hbm.1), custom_call_target="tpu_custom_call" | custom-call | tf_op jit(solution)/shard_map/pallas_call | solution.py:341
  50.9 3.2 %copy.7 = bf16[2,256,2048]{2,1,0:T(8,128)(2,1)} copy(bf16[2,256,2048]{2,1,0:T(8,128)(2,1)} %shard_map.55) | data formatting | bytes 4194304
